TPU v7x, 32 devices: a whole 2x2x4 slice. The times are simulated.
32 devices in a mesh: grid: 8 (over z, x), orb: 4 (over y, core).
Axes of the slice: x: 2, y: 2, z: 4, core: 2. Of those that a mesh axis runs over, the one named last changes fastest.
Arguments:
- orbitals: bfloat16 [1800, 65536], P('orb', 'grid'), may hold values from -0.5 to 1.5
- pivots: int32 [3, 96], replicated, may hold values from 0 to 65535, as said below
Outputs:
- cholesky_factor: float32 [65536, 288], P(('grid', 'orb'))
- residual_diagonal: float32 [65536], P(('grid', 'orb'))
- diagonal_peaks: float32 [3], replicated
Inputs may be any that keep to these rules, and one draw needn't show every extreme that they name: `pivots`: all 3 x 96 pivot indices are distinct grid points.
All inputs are finite; a program needn't handle non-finite values.
Results may differ from a plain program's by a relative error of at most 0.0003.
Values may be sent and summed in bfloat16 or wider, within the bound.
A program may use at most 64 MiB of HBM per device.

v0:
```python
import jax
import jax.numpy as jnp
from jax import lax
from jax.sharding import PartitionSpec as P

ORB = 1800


def pick_columns(values, index, base, count):
    local = index - base
    inside = (local >= 0) & (local < count)
    taken = jnp.take(values, jnp.clip(local, 0, count - 1), axis=1)
    return jnp.where(inside[None, :], taken, jnp.zeros_like(taken))


def contract_first(left, right):
    return lax.dot_general(
        left, right, (((0,), (0,)), ((), ())), preferred_element_type=jnp.float32
    )


def on_device(orbitals, pivots):
    rows = orbitals.shape[1]
    groups = lax.axis_size("orb")
    share = rows // groups
    sections = pivots.shape[0]
    count = pivots.shape[1]
    total_rank = sections * count
    grid_base = lax.axis_index("grid") * rows
    squares = lax.psum_scatter(
        jnp.sum(jnp.square(orbitals.astype(jnp.float32)), axis=0),
        "orb",
        scatter_dimension=0,
        tiled=True,
    )
    diagonal = jnp.square(squares / ORB)
    factor = jnp.zeros((share, total_rank), jnp.float32)
    flat = pivots.reshape(total_rank)
    local_pivots = lax.psum(
        pick_columns(orbitals, flat, grid_base, rows).astype(jnp.float32).astype(jnp.bfloat16),
        "grid",
    )
    whole = lax.all_gather(local_pivots, "orb", axis=0, tiled=True)
    pivot_pairs = contract_first(whole, whole)
    pivot_factor = jnp.zeros((total_rank, total_rank), jnp.float32)
    peaks = []
    for section in range(sections):
        lead = section * count
        sampled_here = lax.slice_in_dim(local_pivots, lead, lead + count, axis=1)
        known = lax.slice_in_dim(pivot_factor, lead, lead + count, axis=0)
        pair = lax.slice_in_dim(
            lax.slice_in_dim(pivot_pairs, lead, lead + count, axis=0), lead, lead + count, axis=1
        )

        def product(start, length, picked=sampled_here):
            return contract_first(orbitals, picked)

        inner = lax.psum_scatter(
            product(jnp.int32(0), share * lax.axis_size("orb")),
            "orb",
            scatter_dimension=0,
            tiled=True,
        )
        block = jnp.square(pair / ORB) - jnp.dot(known, known.T, precision=lax.Precision.HIGHEST)
        columns = jnp.square(inner / ORB) - jnp.dot(
            factor, known.T, precision=lax.Precision.HIGHEST
        )
        lower = jnp.linalg.cholesky(block)
        fresh = jax.scipy.linalg.solve_triangular(lower, columns.T, lower=True).T
        factor = factor.at[:, lead : lead + count].set(fresh)
        pivot_columns = jnp.square(
            lax.slice_in_dim(pivot_pairs, lead, lead + count, axis=1) / ORB
        ) - jnp.dot(pivot_factor, known.T, precision=lax.Precision.HIGHEST)
        pivot_fresh = jax.scipy.linalg.solve_triangular(lower, pivot_columns.T, lower=True).T
        pivot_factor = pivot_factor.at[:, lead : lead + count].set(pivot_fresh)
        diagonal = diagonal - jnp.sum(fresh * fresh, axis=1)
        peaks.append(lax.pmax(jnp.max(diagonal), ("grid", "orb")))
    peak_values = jnp.stack(peaks)
    return (factor, diagonal, peak_values)


def solution(mesh):
    in_specs = (P("orb", "grid"), P())
    out_specs = (P(("grid", "orb"), None), P(("grid", "orb")), P())
    return jax.shard_map(
        on_device, mesh=mesh, in_specs=in_specs, out_specs=out_specs, check_vma=False
    )
```

profile of v0, /device:TPU:0, one launch (start us, length us, event | category | flops | bytes accessed | tf_op | source)
XLA Modules:
  0.0 281.3 jit_solution(3974365267938279486)
XLA Ops:
  7.2 0.7 subtract_clamp_fusion
  8.1 0.7 compare_and_fusion.1
  8.8 11.6 %copy.26 = bf16[450,8192]{0,1:T(8,128)(2,1)} copy(bf16[450,8192]{1,0:T(8,128)(2,1)} %param.17) | data formatting | bytes 14745600 | tf_op args[0]
  20.5 6.5 %gather_fusion = bf16[288,450]{1,0:T(8,128)(2,1)S(1)} fusion(bf16[450,8192]{0,1:T(8,128)(2,1)} %copy.26, s32[1024]{0:T(1024)S(1)} %pad_clamp_fusion), kind=kCustom, calls=%fused_computation | custom fusion | bytes 519552 | tf_op jit(solution)/shard_map/jit(_take)/gather | solution.py:12
  27.0 0.9 select_bitcast_fusion.1
  27.9 74.2 %all-reduce.6.cloned.1.call-done = bf16[450,288]{0,1:T(8,128)(2,1)} async-done(((bf16[450,288]{0,1:T(8,128)(2,1)}), bf16[450,288]{0,1:T(8,128)(2,1)}) %all-reduce.6.cloned.1.call-update) | async-done | bytes 259216 | tf_op jit(solution)/shard_map/psum | solution.py:39
  102.1 6.3 %convolution_bitcast_fusion.2 = f32[8192,96]{0,1:T(8,128)} fusion(bf16[450,8192]{1,0:T(8,128)(2,1)} %param.17, bf16[450,288]{0,1:T(8,128)(2,1)} %all-reduce.6.cloned.1.call-done), kind=kOutput, calls=%fused_computation.4 | convolution fusion | flops 707788800 | bytes 10715136 | tf_op jit(solution)/shard_map/dot_general | solution.py:17
  108.5 0.9 copy-done.2
  109.4 6.4 %convolution_bitcast_fusion.1 = f32[8192,96]{0,1:T(8,128)} fusion(bf16[450,8192]{1,0:T(8,128)(2,1)} %param.17, bf16[450,288]{0,1:T(8,128)(2,1)S(1)} %copy-done.2), kind=kOutput, calls=%fused_computation.3 | convolution fusion | flops 707788800 | bytes 10616832 | tf_op jit(solution)/shard_map/dot_general | solution.py:17
  115.8 6.6 %convolution_bitcast_fusion = f32[8192,96]{0,1:T(8,128)} fusion(bf16[450,8192]{1,0:T(8,128)(2,1)} %param.17, bf16[450,288]{0,1:T(8,128)(2,1)S(1)} %copy-done.2), kind=kOutput, calls=%fused_computation.2 | convolution fusion | flops 707788800 | bytes 10616832 | tf_op jit(solution)/shard_map/dot_general | solution.py:17
  122.5 0.6 copy-done.3
  123.1 0.6 dynamic-slice.43
  124.4 0.6 compare_reduce_fusion.4
  125.0 0.7 compare_reduce_fusion.3
  125.7 4.8 %multiply_reduce_fusion = f32[8192]{0:T(1024)S(1)} fusion(bf16[450,8192]{1,0:T(8,128)(2,1)} %param.17), kind=kLoop, calls=%fused_computation.1 | loop fusion | flops 11051008 | bytes 7405568 | tf_op jit(solution)/shard_map/reduce_sum | solution.py:31
  130.5 12.2 %all-reduce.2 = f32[8192]{0:T(1024)S(1)} all-reduce(f32[8192]{0:T(1024)S(1)} %multiply_reduce_fusion), channel_id=5, replica_groups=mesh['grid'=8,'orb'=4] {'orb'}, use_global_device_ids=true, to_apply=%region_9.13.clone | all-reduce | flops 8192 | bytes 65536
  142.7 10.8 %all-gather = bf16[4,450,288]{1,2,0:T(8,128)(2,1)S(1)} all-gather(bf16[1,450,288]{1,2,0:T(8,128)(2,1)S(1)} %bitcast.91), channel_id=1, replica_groups=mesh['grid'=8,'orb'=4] {'orb'}, dimensions={0}, use_global_device_ids=true | all-gather | bytes 1296000 | tf_op jit(solution)/shard_map/all_gather | solution.py:43
  153.4 0.9 copy.27
  154.3 1.6 reshape.196
  155.9 0.8 fusion.54
  156.9 0.3 convolution_subtract_fusion.5
  157.3 8.8 %cholesky.59 = f32[96,96]{1,0:T(8,128)S(1)} custom-call(f32[96,96]{1,0:T(8,128)S(1)} %fusion.36), custom_call_target="Cholesky" | custom-call | tf_op jit(solution)/shard_map/jit(cholesky)/cholesky | solution.py:68
  166.1 0.6 compare_reduce_fusion.2
  166.7 0.7 fusion.25
  167.4 7.4 %custom-call.11 = f32[1,96,96]{1,2,0:T(8,128)S(1)} custom-call(f32[1,96,96]{2,1,0:T(8,128)S(1)} %fusion.25), custom_call_target="InvertDiagBlocksLowerTriangular" | custom-call | tf_op jit(solution)/shard_map/jit(_solve_triangular)/triangular_solve | solution.py:69
  174.8 1.0 fusion.5
  175.9 0.4 convolution_subtract_fusion.4
  176.4 8.8 %cholesky.70 = f32[96,96]{1,0:T(8,128)S(1)} custom-call(f32[96,96]{1,0:T(8,128)S(1)} %fusion.33), custom_call_target="Cholesky" | custom-call | tf_op jit(solution)/shard_map/jit(cholesky)/cholesky | solution.py:68
  185.2 0.6 compare_reduce_fusion.1
  185.8 0.7 fusion.26
  186.5 7.4 %custom-call.13 = f32[1,96,96]{1,2,0:T(8,128)S(1)} custom-call(f32[1,96,96]{2,1,0:T(8,128)S(1)} %fusion.26), custom_call_target="InvertDiagBlocksLowerTriangular" | custom-call | tf_op jit(solution)/shard_map/jit(_solve_triangular)/triangular_solve | solution.py:69
  194.0 0.6 fusion.2
  194.6 1.0 fusion.4
  195.6 0.6 convolution_subtract_fusion.3
  196.3 8.9 %cholesky.81 = f32[96,96]{1,0:T(8,128)S(1)} custom-call(f32[96,96]{1,0:T(8,128)S(1)} %fusion.29), custom_call_target="Cholesky" | custom-call | tf_op jit(solution)/shard_map/jit(cholesky)/cholesky | solution.py:68
  205.2 0.6 compare_reduce_fusion
  205.9 0.7 fusion.27
  206.5 7.4 %custom-call.15 = f32[1,96,96]{1,2,0:T(8,128)S(1)} custom-call(f32[1,96,96]{2,1,0:T(8,128)S(1)} %fusion.27), custom_call_target="InvertDiagBlocksLowerTriangular" | custom-call | tf_op jit(solution)/shard_map/jit(_solve_triangular)/triangular_solve | solution.py:69
  213.9 2.6 multiply_reduce_fusion.3
  216.9 2.3 fusion.1
  219.2 1.5 bitcast_dynamic-update-slice_fusion
  220.8 5.8 %reduce-scatter.8.cloned.1.call-done = f32[2048,96]{0,1:T(8,128)} async-done(((f32[8192,96]{0,1:T(8,128)}), f32[2048,96]{0,1:T(8,128)}) %reduce-scatter.8.cloned.1.call-update) | async-done | bytes 786448 | tf_op jit(solution)/shard_map/reduce_scatter | solution.py:58
  226.5 3.3 %fusion = f32[96,2048]{1,0:T(8,128)S(1)} fusion(f32[2048,288]{0,1:T(8,128)S(1)} %get-tuple-element.81, f32[2048,96]{0,1:T(8,128)} %reduce-scatter.8.cloned.1.call-done, f32[288,288]{0,1:T(8,128)} %copy-done.1), kind=kOutput, calls=%fused_computation.7 | convolution fusion | flops 680067072 | bytes 4079616 | tf_op jit(solution)/shard_map/dot_general | solution.py:65
  229.9 0.9 multiply_reduce_fusion.1
  230.7 0.8 fusion.46
  231.5 1.2 fusion.48
  232.7 39.6 %all-reduce.3 = (f32[1]{0:T(128)}, f32[1]{0:T(128)}, f32[1]{0:T(128)}) all-reduce(f32[1]{0:T(128)} %bitcast.30, f32[1]{0:T(128)} %bitcast.29, f32[1]{0:T(128)} %bitcast.28), channel_id=1, replica_groups=mesh['grid'=8,'orb'=4] {'grid','orb'}, use_global_device_ids=true, to_apply=%region_18.22 | all-reduce | flops 3 | bytes 24 | tf_op jit(solution)/shard_map/pmax | solution.py:77
  272.3 2.5 pad_maximum_fusion
  (38 shorter events, 1.6 us)
Async XLA Ops:
  7.2 94.9 %all-reduce.6.cloned.1.call-start = ((), (), s32[]{:S(2)}) async-start(), calls=%async_computation.3 | async-start | bytes 589824 | tf_op jit(solution)/shard_map/psum | solution.py:39
  27.9 186.0 %reduce-scatter.4.cloned.1.call-start = ((), (), s32[]{:S(2)}) async-start(), calls=%async_computation.4 | async-start | bytes 3932160 | tf_op jit(solution)/shard_map/reduce_scatter | solution.py:58
  108.4 1.0 copy-start.2
  108.4 108.4 %reduce-scatter.6.cloned.1.call-start = ((), (), s32[]{:S(2)}) async-start(), calls=%async_computation.5 | async-start | bytes 3932160 | tf_op jit(solution)/shard_map/reduce_scatter | solution.py:58
  115.8 110.8 %reduce-scatter.8.cloned.1.call-start = ((), (), s32[]{:S(2)}) async-start(), calls=%async_computation.6 | async-start | bytes 3932160 | tf_op jit(solution)/shard_map/reduce_scatter | solution.py:58
  122.5 0.7 copy-start.3
  195.6 21.0 %copy-start.1 = (f32[288,288]{0,1:T(8,128)}, f32[288,288]{0,1:T(8,128)S(1)}, u32[]{:S(2)}) copy-start(f32[288,288]{0,1:T(8,128)S(1)} %fusion.4) | copy-start | bytes 995332
  230.7 44.1 %copy-start = (f32[2048,288]{0,1:T(8,128)}, f32[2048,288]{0,1:T(8,128)S(1)}, u32[]{:S(2)}) copy-start(f32[2048,288]{0,1:T(8,128)S(1)} %get-tuple-element.77) | copy-start | bytes 7077892
Sparse Core Ops, SparseCore 0:
  28.0 74.0 all-reduce.5
  108.6 37.2 reduce-scatter.3
  148.4 37.8 reduce-scatter.5
  188.7 37.7 reduce-scatter.7
where the time goes:
time: 282 us; the launch traced here: 281 us
  waiting for transfers between devices  80.1 us (28%)
  other arithmetic  65.5 us (23%)
  blocking collectives  62.5 us (22%)
  matrix products  34.5 us (12%)
  local copies, waits for them, and re-layouts  23.8 us (8%)
  between operations  14.8 us (5%)
    psum x1, waiting for transfers between devices, on_device(): lax.psum(pick_columns(orbitals, flat, grid_base, rows).astype(jnp.float32...  74.2 us
    pmax x1, blocking collectives, on_device(): peaks.append(lax.pmax(jnp.max(diagonal), ('grid', 'orb')))  39.6 us
    another operation x9, other arithmetic, on_device(): lower = jnp.linalg.cholesky(block)  28.5 us
    another operation x6, other arithmetic, on_device(): fresh = jax.scipy.linalg.solve_triangular(lower, columns.T, lower=True).T  24 us
    dot_general x4, matrix products, contract_first(): lax.dot_general(left, right, (((0,), (0,)), ((), ())), preferred_element_...  20.1 us
    unnamed x14, local copies, waits for them, and re-layouts  15.5 us
    unnamed x1, blocking collectives  12.2 us
    all_gather x1, blocking collectives, on_device(): whole = lax.all_gather(local_pivots, 'orb', axis=0, tiled=True)  10.8 us
  transfers between devices with their start and end apart: 4, of which 2 were waited for; matrix products, arithmetic and copies ran while one was open for 31% of the time, Pallas kernels for 0%

commit v1 on v0

--- a/solution.py
+++ b/solution.py
@@ -36,10 +36,9 @@
     diagonal = jnp.square(squares / ORB)
     factor = jnp.zeros((share, total_rank), jnp.float32)
     flat = pivots.reshape(total_rank)
-    local_pivots = lax.psum(
-        pick_columns(orbitals, flat, grid_base, rows).astype(jnp.float32).astype(jnp.bfloat16),
-        "grid",
-    )
+    part = pick_columns(orbitals, flat, grid_base, rows).astype(jnp.float32).astype(jnp.bfloat16)
+    blocks = lax.all_gather(part, "grid", axis=0, tiled=False)
+    local_pivots = blocks.sum(axis=0)
     whole = lax.all_gather(local_pivots, "orb", axis=0, tiled=True)
     pivot_pairs = contract_first(whole, whole)
     pivot_factor = jnp.zeros((total_rank, total_rank), jnp.float32)

time: 282 us -> 265 us (0.940)
  waiting for transfers between devices: 80.1 us -> 61.1 us
    psum x1 -> x0, waiting for transfers between devices: 74.2 us -> none  [on_device(): lax.psum(pick_columns(orbitals, flat, grid_base, rows).astype(jnp.float32...]
    all_gather x0 -> x1, waiting for transfers between devices: none -> 54.6 us  [on_device(): blocks = lax.all_gather(part, 'grid', axis=0, tiled=False)]
    unnamed x14 -> x12, local copies, waits for them, and re-layouts: 15.5 us -> 14.7 us
  transfers between devices with their start and end apart: 4 -> 4, of which waited for: 2 -> 2; matrix products, arithmetic and copies ran while one was open for 31% -> 33% of each run, Pallas kernels for 0% -> 0%
where the time goes in v1:
time: 265 us; the launch traced here: 264 us
  other arithmetic  67.6 us (26%)
  blocking collectives  62.5 us (24%)
  waiting for transfers between devices  61.1 us (23%)
  matrix products  34.6 us (13%)
  local copies, waits for them, and re-layouts  22.9 us (9%)
  between operations  14.8 us (6%)
    all_gather x1, waiting for transfers between devices, on_device(): blocks = lax.all_gather(part, 'grid', axis=0, tiled=False)  54.6 us
    pmax x1, blocking collectives, on_device(): peaks.append(lax.pmax(jnp.max(diagonal), ('grid', 'orb')))  39.5 us
    another operation x9, other arithmetic, on_device(): lower = jnp.linalg.cholesky(block)  28.5 us
    another operation x6, other arithmetic, on_device(): fresh = jax.scipy.linalg.solve_triangular(lower, columns.T, lower=True).T  24 us
    dot_general x4, matrix products, contract_first(): lax.dot_general(left, right, (((0,), (0,)), ((), ())), preferred_element_...  20.2 us
    unnamed x12, local copies, waits for them, and re-layouts  14.7 us
    unnamed x1, blocking collectives  12.3 us
    all_gather x1, blocking collectives, on_device(): whole = lax.all_gather(local_pivots, 'orb', axis=0, tiled=True)  10.7 us
  transfers between devices with their start and end apart: 4, of which 2 were waited for; matrix products, arithmetic and copies ran while one was open for 33% of the time, Pallas kernels for 0%

profile of v1, /device:TPU:0, one launch (start us, length us, event | category | flops | bytes accessed | tf_op | source)
XLA Modules:
  0.0 263.7 jit_solution(13357998127385898650)
XLA Ops:
  7.2 0.7 subtract_clamp_fusion
  8.1 0.7 compare_and_fusion.1
  8.8 11.6 %copy.36 = bf16[450,8192]{0,1:T(8,128)(2,1)} copy(bf16[450,8192]{1,0:T(8,128)(2,1)} %param.17) | data formatting | bytes 14745600 | tf_op args[0]
  20.5 6.5 %gather_fusion = bf16[288,450]{1,0:T(8,128)(2,1)S(1)} fusion(bf16[450,8192]{0,1:T(8,128)(2,1)} %copy.36, s32[1024]{0:T(1024)S(1)} %pad_clamp_fusion), kind=kCustom, calls=%fused_computation | custom fusion | bytes 519552 | tf_op jit(solution)/shard_map/jit(_take)/gather | solution.py:12
  27.0 0.9 fusion.12
  27.9 54.6 %all-gather.3.cloned.1.call-done = bf16[8,450,288]{1,2,0:T(8,128)(2,1)} async-done(((bf16[1,450,288]{1,2,0:T(8,128)(2,1)}), bf16[8,450,288]{1,2,0:T(8,128)(2,1)}) %all-gather.3.cloned.1.call-update) | async-done | bytes 2073616 | tf_op jit(solution)/shard_map/all_gather | solution.py:40
  82.6 2.1 reduce_sum.48
  84.7 6.3 %convolution_bitcast_fusion.2 = f32[8192,96]{0,1:T(8,128)} fusion(bf16[450,8192]{1,0:T(8,128)(2,1)} %param.17, bf16[450,288]{0,1:T(8,128)(2,1)S(1)} %reduce_sum.48), kind=kOutput, calls=%fused_computation.4 | convolution fusion | flops 707788800 | bytes 10616832 | tf_op jit(solution)/shard_map/dot_general | solution.py:17
  91.1 6.3 %convolution_bitcast_fusion.1 = f32[8192,96]{0,1:T(8,128)} fusion(bf16[450,8192]{1,0:T(8,128)(2,1)} %param.17, bf16[450,288]{0,1:T(8,128)(2,1)S(1)} %reduce_sum.48), kind=kOutput, calls=%fused_computation.3 | convolution fusion | flops 707788800 | bytes 10616832 | tf_op jit(solution)/shard_map/dot_general | solution.py:17
  97.5 6.8 %convolution_bitcast_fusion = f32[8192,96]{0,1:T(8,128)} fusion(bf16[450,8192]{1,0:T(8,128)(2,1)} %param.17, bf16[450,288]{0,1:T(8,128)(2,1)S(1)} %reduce_sum.48), kind=kOutput, calls=%fused_computation.2 | convolution fusion | flops 707788800 | bytes 10616832 | tf_op jit(solution)/shard_map/dot_general | solution.py:17
  104.3 0.6 copy-done.2
  104.9 0.6 dynamic-slice.43
  106.2 0.6 compare_reduce_fusion.4
  106.8 0.7 compare_reduce_fusion.3
  107.5 4.8 %multiply_reduce_fusion = f32[8192]{0:T(1024)S(1)} fusion(bf16[450,8192]{1,0:T(8,128)(2,1)} %param.17), kind=kLoop, calls=%fused_computation.1 | loop fusion | flops 11051008 | bytes 7405568 | tf_op jit(solution)/shard_map/reduce_sum | solution.py:31
  112.3 12.3 %all-reduce.2 = f32[8192]{0:T(1024)S(1)} all-reduce(f32[8192]{0:T(1024)S(1)} %multiply_reduce_fusion), channel_id=5, replica_groups=mesh['grid'=8,'orb'=4] {'orb'}, use_global_device_ids=true, to_apply=%region_9.13.clone | all-reduce | flops 8192 | bytes 65536
  124.6 10.7 %all-gather = bf16[4,450,288]{1,2,0:T(8,128)(2,1)S(1)} all-gather(bf16[1,450,288]{1,2,0:T(8,128)(2,1)S(1)} %bitcast.95), channel_id=1, replica_groups=mesh['grid'=8,'orb'=4] {'orb'}, dimensions={0}, use_global_device_ids=true | all-gather | bytes 1296000 | tf_op jit(solution)/shard_map/all_gather | solution.py:42
  135.3 0.9 copy.37
  136.2 1.6 reshape.247
  137.8 0.8 fusion.55
  138.8 0.3 convolution_subtract_fusion.5
  139.2 8.8 %cholesky.59 = f32[96,96]{1,0:T(8,128)S(1)} custom-call(f32[96,96]{1,0:T(8,128)S(1)} %fusion.37), custom_call_target="Cholesky" | custom-call | tf_op jit(solution)/shard_map/jit(cholesky)/cholesky | solution.py:67
  148.0 0.6 compare_reduce_fusion.2
  148.6 0.7 fusion.26
  149.3 7.4 %custom-call.11 = f32[1,96,96]{1,2,0:T(8,128)S(1)} custom-call(f32[1,96,96]{2,1,0:T(8,128)S(1)} %fusion.26), custom_call_target="InvertDiagBlocksLowerTriangular" | custom-call | tf_op jit(solution)/shard_map/jit(_solve_triangular)/triangular_solve | solution.py:68
  156.7 1.0 fusion.5
  157.8 0.4 convolution_subtract_fusion.4
  158.3 8.8 %cholesky.70 = f32[96,96]{1,0:T(8,128)S(1)} custom-call(f32[96,96]{1,0:T(8,128)S(1)} %fusion.34), custom_call_target="Cholesky" | custom-call | tf_op jit(solution)/shard_map/jit(cholesky)/cholesky | solution.py:67
  167.1 0.6 compare_reduce_fusion.1
  167.7 0.7 fusion.27
  168.4 7.4 %custom-call.13 = f32[1,96,96]{1,2,0:T(8,128)S(1)} custom-call(f32[1,96,96]{2,1,0:T(8,128)S(1)} %fusion.27), custom_call_target="InvertDiagBlocksLowerTriangular" | custom-call | tf_op jit(solution)/shard_map/jit(_solve_triangular)/triangular_solve | solution.py:68
  175.9 0.6 fusion.2
  176.5 1.0 fusion.4
  177.5 0.6 convolution_subtract_fusion.3
  178.2 8.9 %cholesky.81 = f32[96,96]{1,0:T(8,128)S(1)} custom-call(f32[96,96]{1,0:T(8,128)S(1)} %fusion.30), custom_call_target="Cholesky" | custom-call | tf_op jit(solution)/shard_map/jit(cholesky)/cholesky | solution.py:67
  187.1 0.6 compare_reduce_fusion
  187.8 0.7 fusion.28
  188.4 7.4 %custom-call.15 = f32[1,96,96]{1,2,0:T(8,128)S(1)} custom-call(f32[1,96,96]{2,1,0:T(8,128)S(1)} %fusion.28), custom_call_target="InvertDiagBlocksLowerTriangular" | custom-call | tf_op jit(solution)/shard_map/jit(_solve_triangular)/triangular_solve | solution.py:68
  195.8 2.6 %multiply_reduce_fusion.3 = (f32[2048]{0:T(1024)S(1)}, f32[2048,96]{0,1:T(8,128)S(1)}) fusion(pred[]{:T(512)} %compare_reduce_fusion.4, f32[2048,96]{0,1:T(8,128)} %reduce-scatter.4.cloned.1.call-done, f32[1,96,96]{1,2,0:T(8,128)S(1)} %custom-call.11), kind=kOutput, calls=%fused_computation.25 | convolution fusion | flops 227473408 | bytes 1617921 | tf_op jit(solution)/shard_map/jit(_solve_triangular)/triangular_solve | solution.py:68
  198.8 2.3 fusion.1
  201.1 1.5 bitcast_dynamic-update-slice_fusion
  202.7 6.3 %reduce-scatter.8.cloned.1.call-done = f32[2048,96]{0,1:T(8,128)} async-done(((f32[8192,96]{0,1:T(8,128)}), f32[2048,96]{0,1:T(8,128)}) %reduce-scatter.8.cloned.1.call-update) | async-done | bytes 786448 | tf_op jit(solution)/shard_map/reduce_scatter | solution.py:57
  209.0 3.3 %fusion = f32[96,2048]{1,0:T(8,128)S(1)} fusion(f32[2048,288]{0,1:T(8,128)S(1)} %get-tuple-element.81, f32[2048,96]{0,1:T(8,128)} %reduce-scatter.8.cloned.1.call-done, f32[288,288]{0,1:T(8,128)} %copy-done.1), kind=kOutput, calls=%fused_computation.7 | convolution fusion | flops 680067072 | bytes 4079616 | tf_op jit(solution)/shard_map/dot_general | solution.py:64
  212.3 0.9 multiply_reduce_fusion.1
  213.2 0.8 fusion.47
  214.0 1.2 fusion.49
  215.2 39.5 %all-reduce.3 = (f32[1]{0:T(128)}, f32[1]{0:T(128)}, f32[1]{0:T(128)}) all-reduce(f32[1]{0:T(128)} %bitcast.31, f32[1]{0:T(128)} %bitcast.30, f32[1]{0:T(128)} %bitcast.29), channel_id=1, replica_groups=mesh['grid'=8,'orb'=4] {'grid','orb'}, use_global_device_ids=true, to_apply=%region_18.22 | all-reduce | flops 3 | bytes 24 | tf_op jit(solution)/shard_map/pmax | solution.py:76
  254.7 2.5 pad_maximum_fusion
  (37 shorter events, 1.6 us)
Async XLA Ops:
  7.2 75.4 %all-gather.3.cloned.1.call-start = ((), (), s32[]{:S(2)}) async-start(), calls=%async_computation.3 | async-start | bytes 2654208 | tf_op jit(solution)/shard_map/all_gather | solution.py:40
  27.9 167.9 %reduce-scatter.4.cloned.1.call-start = ((), (), s32[]{:S(2)}) async-start(), calls=%async_computation.4 | async-start | bytes 3932160 | tf_op jit(solution)/shard_map/reduce_scatter | solution.py:57
  91.0 107.7 %reduce-scatter.6.cloned.1.call-start = ((), (), s32[]{:S(2)}) async-start(), calls=%async_computation.5 | async-start | bytes 3932160 | tf_op jit(solution)/shard_map/reduce_scatter | solution.py:57
  97.4 111.5 %reduce-scatter.8.cloned.1.call-start = ((), (), s32[]{:S(2)}) async-start(), calls=%async_computation.6 | async-start | bytes 3932160 | tf_op jit(solution)/shard_map/reduce_scatter | solution.py:57
  104.3 0.7 copy-start.2
  177.5 21.0 %copy-start.1 = (f32[288,288]{0,1:T(8,128)}, f32[288,288]{0,1:T(8,128)S(1)}, u32[]{:S(2)}) copy-start(f32[288,288]{0,1:T(8,128)S(1)} %fusion.4) | copy-start | bytes 995332
  213.2 44.0 %copy-start = (f32[2048,288]{0,1:T(8,128)}, f32[2048,288]{0,1:T(8,128)S(1)}, u32[]{:S(2)}) copy-start(f32[2048,288]{0,1:T(8,128)S(1)} %get-tuple-element.77) | copy-start | bytes 7077892
Sparse Core Ops, SparseCore 0:
  28.0 54.5 all-gather.2
  91.2 36.7 reduce-scatter.3
  130.5 38.0 reduce-scatter.5
  171.1 37.8 reduce-scatter.7
